TPU v7x, 32 devices: a whole 2x2x4 slice. The times are simulated.
32 devices in a mesh: req: 2 (over y), blk: 4 (over z), uly: 4 (over x, core).
Axes of the slice: x: 2, y: 2, z: 4, core: 2. Of those that a mesh axis runs over, the one named last changes fastest.
Arguments:
- video_qkv: bfloat16 [3, 2048, 3072], P(None, ('req', 'blk', 'uly')), parts along dimension 1, may hold values from -16 to 16
- text_qkv: bfloat16 [3, 64, 3072], P(None, ('req', 'blk', 'uly')), parts along dimension 1, may hold values from -9.5625 to 9.5625
- video_gate: float32 [6144], P('req'), parts along dimension 0, may hold values from 1 to 4
- text_gate: float32 [6144], P('req'), parts along dimension 0, may hold values from 1 to 4
Outputs:
- video_out: bfloat16 [2048, 3072], P(('req', 'blk', 'uly')), parts along dimension 0
- text_out: bfloat16 [64, 3072], P(('req', 'blk', 'uly')), parts along dimension 0
There are 2 independent parts, one for each index of `req`. A program takes and returns all parts, laid end to end along the dimension named above; each array names one. Nothing has to cross between parts.
All inputs are finite; a program needn't handle non-finite values.
Results may differ from a plain program's by a relative error of at most 0.0085.
Values may be sent and summed in bfloat16 or wider, within the bound.
No kernel may reach another device: no remote copies, remote signals or barrier semaphores. Data moves between devices by JAX's collectives and lax.ppermute only.
A program may use at most 128 MiB of HBM per device.

v0:
```python
import math

import jax
import jax.numpy as jnp
from jax import lax
from jax.sharding import PartitionSpec as P

HEADS = 24
HD = 128


def merge_block(state, queries, block_pair):
    best, total, summed = state
    scale = 1.0 / math.sqrt(queries.shape[-1])
    scores = (
        jnp.einsum("qhd,khd->hqk", queries, block_pair[0], preferred_element_type=jnp.float32)
        * scale
    )
    new_best = jnp.maximum(best, jnp.max(scores, axis=2))
    factor = jnp.exp(best - new_best)
    raised = jnp.exp(scores - new_best[:, :, None])
    total = total * factor + jnp.sum(raised, axis=2)
    product = jnp.einsum(
        "hqk,khd->hqd",
        raised.astype(jnp.bfloat16),
        block_pair[1],
        preferred_element_type=jnp.float32,
    )
    summed = summed * factor[:, :, None] + product
    return (new_best, total, summed)


def attend(video_heads, text_heads):
    heads = video_heads.shape[3]
    width = video_heads.shape[4]
    rows_video = video_heads.shape[1]
    rows_text = text_heads.shape[1]
    joined = jnp.concatenate((video_heads, text_heads), axis=1)
    rows_all = rows_video + rows_text
    joined = joined.reshape(3, rows_all, heads, width)
    queries = joined[0]
    key_pairs = joined[1:]
    initial = (
        jnp.full((heads, rows_all), -jnp.inf, jnp.float32),
        jnp.zeros((heads, rows_all), jnp.float32),
        jnp.zeros((heads, rows_all, width), jnp.float32),
    )
    piece = lax.all_gather(key_pairs, "blk", axis=1, tiled=True)
    count = piece.shape[1] // rows_all

    def one_block(index, inner):
        block_pair = lax.dynamic_slice_in_dim(piece, index * rows_all, rows_all, 1)
        return merge_block(inner, queries, block_pair)

    best, total, summed = lax.fori_loop(0, count, one_block, initial)
    attended = (summed / total[:, :, None]).transpose(1, 0, 2).astype(jnp.bfloat16)
    video_att = attended[:rows_video].reshape(rows_video, 1, heads, width)
    text_att = attended[rows_video:].reshape(rows_text, 1, heads, width)
    return (video_att, text_att)


def on_device(video_qkv, text_qkv, video_gate, text_gate):
    groups = lax.axis_size("uly")
    local_heads = HEADS // groups
    video_rows = video_qkv.shape[1]
    text_rows = text_qkv.shape[1]
    video_split = video_qkv.reshape(3, video_rows, groups, local_heads, HD)
    text_split = text_qkv.reshape(3, text_rows, groups, local_heads, HD)
    video_heads, text_heads = (
        lax.all_to_all(video_split, "uly", split_axis=2, concat_axis=1, tiled=True),
        lax.all_to_all(text_split, "uly", split_axis=2, concat_axis=1, tiled=True),
    )
    video_att, text_att = attend(video_heads, text_heads)
    video_back, text_back = (
        lax.all_to_all(video_att, "uly", split_axis=0, concat_axis=1, tiled=True),
        lax.all_to_all(text_att, "uly", split_axis=0, concat_axis=1, tiled=True),
    )
    video_flat = video_back.reshape(video_rows, HEADS * HD).astype(jnp.float32)
    text_flat = text_back.reshape(text_rows, HEADS * HD).astype(jnp.float32)
    video_out = (video_flat * video_gate[None, :]).astype(jnp.bfloat16)
    text_out = (text_flat * text_gate[None, :]).astype(jnp.bfloat16)
    return (video_out, text_out)


def solution(mesh):
    in_specs = (
        P(None, ("req", "blk", "uly"), None),
        P(None, ("req", "blk", "uly"), None),
        P("req"),
        P("req"),
    )
    out_specs = (P(("req", "blk", "uly"), None), P(("req", "blk", "uly"), None))
    return jax.shard_map(
        on_device, mesh=mesh, in_specs=in_specs, out_specs=out_specs, check_vma=False
    )
```

profile of v0, /device:TPU:0, one launch (start us, length us, event | category | flops | bytes accessed | tf_op | source)
XLA Modules:
  0.0 148.8 jit_solution(10764639887761051975)
XLA Ops:
  7.2 0.8 reshape.38
  8.0 0.6 copy.22
  8.6 4.2 %all-to-all-start.1 = ((bf16[3,2,4,6,128]{4,1,3,0,2:T(2,128)(2,1)}), bf16[3,2,4,6,128]{4,1,3,0,2:T(2,128)(2,1)S(1)}, u32[]{:S(2)}, u32[]{:S(2)}) async-start(bf16[3,2,4,6,128]{4,1,3,0,2:T(2,128)(2,1)} %copy.22), calls=%async_computation.1 | async-start | bytes 73728 | tf_op jit(solution)/shard_map/all_to_all | solution.py:71
  12.9 2.8 %reshape.37 = bf16[3,64,4,6,128]{4,3,2,1,0:T(8,128)(2,1)S(1)} reshape(bf16[3,64,3072]{2,1,0:T(8,128)(2,1)} %param.6) | data formatting | bytes 2359296 | tf_op jit(solution)/shard_map/reshape | solution.py:67
  15.7 1.5 copy.20
  17.2 3.5 %all-to-all-start = ((bf16[3,64,4,6,128]{4,1,3,0,2:T(8,128)(2,1)}), bf16[3,64,4,6,128]{4,1,3,0,2:T(8,128)(2,1)S(1)}, u32[]{:S(2)}, u32[]{:S(2)}) async-start(bf16[3,64,4,6,128]{4,1,3,0,2:T(8,128)(2,1)} %copy.20), calls=%async_computation | async-start | bytes 2359296 | tf_op jit(solution)/shard_map/all_to_all | solution.py:70
  20.8 15.7 %all-to-all-done = bf16[3,64,4,6,128]{4,1,3,0,2:T(8,128)(2,1)S(1)} async-done(((bf16[3,64,4,6,128]{4,1,3,0,2:T(8,128)(2,1)}), bf16[3,64,4,6,128]{4,1,3,0,2:T(8,128)(2,1)S(1)}, u32[]{:S(2)}, u32[]{:S(2)}) %all-to-all-start) | async-done | bytes 1179680 | tf_op jit(solution)/shard_map/all_to_all | solution.py:70
  36.6 1.0 fusion.12
  37.7 66.0 %all-gather.3.cloned.1.call-done = bf16[2,1056,1,6,128]{4,1,3,0,2:T(8,128)(2,1)} async-done(((bf16[2,264,1,6,128]{4,1,3,0,2:T(8,128)(2,1)}), bf16[2,1056,1,6,128]{4,1,3,0,2:T(8,128)(2,1)}) %all-gather.3.cloned.1.call-update) | async-done | bytes 3244048 | tf_op jit(solution)/shard_map/all_gather | solution.py:48
  103.7 16.6 %while.18 = (s32[]{:T(128)}, f32[6,264]{1,0:T(8,128)S(1)}, f32[6,264]{1,0:T(8,128)S(1)}, f32[6,264,128]{2,1,0:T(8,128)S(1)}, bf16[2,1056,6,128]{3,1,2,0:T(8,128)...) while((s32[]{:T(128)}, f32[6,264]{1,0:T(8,128)S(1)}, ...), condition=%wide.region_3.0_spmd.clone, body=%wide.region_0.0_spmd.clone.sunk | while | flops 218067712 | bytes 7958215 | solution.py:55
  103.7 1.6 %bitcast_reduce_fusion.2 = (f32[6,264]{1,0:T(8,128)S(1)}, f32[6,264,264]{2,1,0:T(8,128)S(1)}) fusion(bf16[264,6,128]{2,0,1:T(8,128)(2,1)S(1)} %get-tuple-element.223, bf16[2,1056,6,128]{3,1,2,0:T(8,128)(2,1)} %get-tuple-element.222, s32[]{:T(128)S(6)} %select_n.9), kind=kOutput, calls=%fused_computation.1.clone.1 | convolution fusion | flops 107887824 | bytes 2490052 | tf_op jit(solution)/shard_map/while/body/eval_jaxpr/qhd,khd->hqk/dot_general | solution.py:16
  105.3 0.4 fusion.24
  105.8 2.0 %convolution_add_fusion.2 = f32[6,264,128]{2,1,0:T(8,128)S(1)} fusion(f32[6,264,264]{2,1,0:T(8,128)S(1)} %get-tuple-element.193, f32[6,264]{1,0:T(8,128)S(1)} %select_maximum_fusion.2, f32[6,264,128]{2,1,0:T(8,128)S(1)} %get-tuple-element.210, bf16[2,1056,6,128]{3,1,2,0:T(8,128)(2,1)} %get-tuple-element.222, s32[]{:T(128)S(6)} %add.53, ...), kind=kOutput, calls=%fused_computation.5.clone.1 | convolution fusion | flops 108915840 | bytes 3712905 | tf_op jit(solution)/shard_map/while/body/eval_jaxpr/hqk,khd->hqd/dot_general | solution.py:23
  107.8 1.6 %bitcast_reduce_fusion.2 = (f32[6,264]{1,0:T(8,128)S(1)}, f32[6,264,264]{2,1,0:T(8,128)S(1)}) fusion(bf16[264,6,128]{2,0,1:T(8,128)(2,1)S(1)} %get-tuple-element.223, bf16[2,1056,6,128]{3,1,2,0:T(8,128)(2,1)} %get-tuple-element.222, s32[]{:T(128)S(6)} %select_n.9), kind=kOutput, calls=%fused_computation.1.clone.1 | convolution fusion | flops 107887824 | bytes 2490052 | tf_op jit(solution)/shard_map/while/body/eval_jaxpr/qhd,khd->hqk/dot_general | solution.py:16
  109.5 0.4 fusion.24
  109.9 2.0 %convolution_add_fusion.2 = f32[6,264,128]{2,1,0:T(8,128)S(1)} fusion(f32[6,264,264]{2,1,0:T(8,128)S(1)} %get-tuple-element.193, f32[6,264]{1,0:T(8,128)S(1)} %select_maximum_fusion.2, f32[6,264,128]{2,1,0:T(8,128)S(1)} %get-tuple-element.210, bf16[2,1056,6,128]{3,1,2,0:T(8,128)(2,1)} %get-tuple-element.222, s32[]{:T(128)S(6)} %add.53, ...), kind=kOutput, calls=%fused_computation.5.clone.1 | convolution fusion | flops 108915840 | bytes 3712905 | tf_op jit(solution)/shard_map/while/body/eval_jaxpr/hqk,khd->hqd/dot_general | solution.py:23
  112.0 1.6 %bitcast_reduce_fusion.2 = (f32[6,264]{1,0:T(8,128)S(1)}, f32[6,264,264]{2,1,0:T(8,128)S(1)}) fusion(bf16[264,6,128]{2,0,1:T(8,128)(2,1)S(1)} %get-tuple-element.223, bf16[2,1056,6,128]{3,1,2,0:T(8,128)(2,1)} %get-tuple-element.222, s32[]{:T(128)S(6)} %select_n.9), kind=kOutput, calls=%fused_computation.1.clone.1 | convolution fusion | flops 107887824 | bytes 2490052 | tf_op jit(solution)/shard_map/while/body/eval_jaxpr/qhd,khd->hqk/dot_general | solution.py:16
  113.6 0.4 fusion.24
  114.1 2.0 %convolution_add_fusion.2 = f32[6,264,128]{2,1,0:T(8,128)S(1)} fusion(f32[6,264,264]{2,1,0:T(8,128)S(1)} %get-tuple-element.193, f32[6,264]{1,0:T(8,128)S(1)} %select_maximum_fusion.2, f32[6,264,128]{2,1,0:T(8,128)S(1)} %get-tuple-element.210, bf16[2,1056,6,128]{3,1,2,0:T(8,128)(2,1)} %get-tuple-element.222, s32[]{:T(128)S(6)} %add.53, ...), kind=kOutput, calls=%fused_computation.5.clone.1 | convolution fusion | flops 108915840 | bytes 3712905 | tf_op jit(solution)/shard_map/while/body/eval_jaxpr/hqk,khd->hqd/dot_general | solution.py:23
  116.2 1.6 %bitcast_reduce_fusion.2 = (f32[6,264]{1,0:T(8,128)S(1)}, f32[6,264,264]{2,1,0:T(8,128)S(1)}) fusion(bf16[264,6,128]{2,0,1:T(8,128)(2,1)S(1)} %get-tuple-element.223, bf16[2,1056,6,128]{3,1,2,0:T(8,128)(2,1)} %get-tuple-element.222, s32[]{:T(128)S(6)} %select_n.9), kind=kOutput, calls=%fused_computation.1.clone.1 | convolution fusion | flops 107887824 | bytes 2490052 | tf_op jit(solution)/shard_map/while/body/eval_jaxpr/qhd,khd->hqk/dot_general | solution.py:16
  117.8 0.4 fusion.24
  118.3 2.0 %convolution_add_fusion.2 = f32[6,264,128]{2,1,0:T(8,128)S(1)} fusion(f32[6,264,264]{2,1,0:T(8,128)S(1)} %get-tuple-element.193, f32[6,264]{1,0:T(8,128)S(1)} %select_maximum_fusion.2, f32[6,264,128]{2,1,0:T(8,128)S(1)} %get-tuple-element.210, bf16[2,1056,6,128]{3,1,2,0:T(8,128)(2,1)} %get-tuple-element.222, s32[]{:T(128)S(6)} %add.53, ...), kind=kOutput, calls=%fused_computation.5.clone.1 | convolution fusion | flops 108915840 | bytes 3712905 | tf_op jit(solution)/shard_map/while/body/eval_jaxpr/hqk,khd->hqd/dot_general | solution.py:23
  120.5 0.4 fusion.13
  120.8 0.6 slice_bitcast_fusion.1
  121.4 3.3 %all-to-all-start.3 = ((bf16[8,1,6,128]{3,2,1,0:T(8,128)(2,1)}), bf16[8,1,6,128]{3,2,1,0:T(8,128)(2,1)S(1)}, u32[]{:S(2)}, u32[]{:S(2)}) async-start(bf16[8,1,6,128]{3,2,1,0:T(8,128)(2,1)} %slice_bitcast_fusion.1), calls=%async_computation.3 | async-start | bytes 32768 | tf_op jit(solution)/shard_map/all_to_all | solution.py:76
  124.7 0.8 slice_bitcast_fusion
  125.5 3.0 %all-to-all-done.3 = bf16[8,1,6,128]{3,2,1,0:T(8,128)(2,1)S(1)} async-done(((bf16[8,1,6,128]{3,2,1,0:T(8,128)(2,1)}), bf16[8,1,6,128]{3,2,1,0:T(8,128)(2,1)S(1)}, u32[]{:S(2)}, u32[]{:S(2)}) %all-to-all-start.3) | async-done | bytes 12320 | tf_op jit(solution)/shard_map/all_to_all | solution.py:76
  128.5 3.5 %all-to-all-start.2 = ((bf16[256,1,6,128]{3,2,1,0:T(8,128)(2,1)}), bf16[256,1,6,128]{3,2,1,0:T(8,128)(2,1)S(1)}, u32[]{:S(2)}, u32[]{:S(2)}) async-start(bf16[256,1,6,128]{3,2,1,0:T(8,128)(2,1)} %slice_bitcast_fusion), calls=%async_computation.2 | async-start | bytes 1048576 | tf_op jit(solution)/shard_map/all_to_all | solution.py:75
  132.0 0.6 multiply_convert_fusion.1
  132.7 8.1 %all-to-all-done.2 = bf16[256,1,6,128]{3,2,1,0:T(8,128)(2,1)S(1)} async-done(((bf16[256,1,6,128]{3,2,1,0:T(8,128)(2,1)}), bf16[256,1,6,128]{3,2,1,0:T(8,128)(2,1)S(1)}, u32[]{:S(2)}, u32[]{:S(2)}) %all-to-all-start.2) | async-done | bytes 393248 | tf_op jit(solution)/shard_map/all_to_all | solution.py:75
  140.9 0.2 reshape.41
  141.1 0.8 multiply_convert_fusion
  (29 shorter events, 0.6 us)
Async XLA Ops:
  8.6 8.6 %all-to-all-start.1 = ((bf16[3,2,4,6,128]{4,1,3,0,2:T(2,128)(2,1)}), bf16[3,2,4,6,128]{4,1,3,0,2:T(2,128)(2,1)S(1)}, u32[]{:S(2)}, u32[]{:S(2)}) async-start(bf16[3,2,4,6,128]{4,1,3,0,2:T(2,128)(2,1)} %copy.22), calls=%async_computation.1 | async-start | bytes 73728 | tf_op jit(solution)/shard_map/all_to_all | solution.py:71
  17.2 19.3 %all-to-all-start = ((bf16[3,64,4,6,128]{4,1,3,0,2:T(8,128)(2,1)}), bf16[3,64,4,6,128]{4,1,3,0,2:T(8,128)(2,1)S(1)}, u32[]{:S(2)}, u32[]{:S(2)}) async-start(bf16[3,64,4,6,128]{4,1,3,0,2:T(8,128)(2,1)} %copy.20), calls=%async_computation | async-start | bytes 2359296 | tf_op jit(solution)/shard_map/all_to_all | solution.py:70
  20.7 83.0 %all-gather.3.cloned.1.call-start = ((), (), s32[]{:S(2)}) async-start(), calls=%async_computation.4 | async-start | bytes 4055040 | tf_op jit(solution)/shard_map/all_gather | solution.py:48
  120.3 11.7 %copy-start.1 = (f32[3072]{0:T(1024)S(1)}, f32[3072]{0:T(1024)}, u32[]{:S(2)}) copy-start(f32[3072]{0:T(1024)} %param.9) | copy-start | bytes 36868
  121.4 7.1 %all-to-all-start.3 = ((bf16[8,1,6,128]{3,2,1,0:T(8,128)(2,1)}), bf16[8,1,6,128]{3,2,1,0:T(8,128)(2,1)S(1)}, u32[]{:S(2)}, u32[]{:S(2)}) async-start(bf16[8,1,6,128]{3,2,1,0:T(8,128)(2,1)} %slice_bitcast_fusion.1), calls=%async_computation.3 | async-start | bytes 32768 | tf_op jit(solution)/shard_map/all_to_all | solution.py:76
  125.5 15.6 %copy-start = (f32[3072]{0:T(1024)S(1)}, f32[3072]{0:T(1024)}, u32[]{:S(2)}) copy-start(f32[3072]{0:T(1024)} %param.8) | copy-start | bytes 36868
  128.5 12.3 %all-to-all-start.2 = ((bf16[256,1,6,128]{3,2,1,0:T(8,128)(2,1)}), bf16[256,1,6,128]{3,2,1,0:T(8,128)(2,1)S(1)}, u32[]{:S(2)}, u32[]{:S(2)}) async-start(bf16[256,1,6,128]{3,2,1,0:T(8,128)(2,1)} %slice_bitcast_fusion), calls=%async_computation.2 | async-start | bytes 1048576 | tf_op jit(solution)/shard_map/all_to_all | solution.py:75
Sparse Core Ops, SparseCore 0:
  37.7 65.8 all-gather.2
where the time goes:
time: 150 us; the launch traced here: 149 us
  waiting for transfers between devices  92.8 us (62%)
  starting transfers between devices  14.5 us (10%)
  matrix products  14.5 us (10%)
  between operations  14.2 us (9%)
  local copies, waits for them, and re-layouts  7.71 us (5%)
  other arithmetic  4.76 us (3%)
    all_gather x1, waiting for transfers between devices, attend(): piece = lax.all_gather(key_pairs, 'blk', axis=1, tiled=True)  66 us
    all_to_all x1, waiting for transfers between devices, on_device(): lax.all_to_all(video_split, 'uly', split_axis=2, concat_axis=1, tiled=True)  15.7 us
    all_to_all x1, waiting for transfers between devices, on_device(): lax.all_to_all(video_att, 'uly', split_axis=0, concat_axis=1, tiled=True)  8.12 us
    dot_general x4, matrix products, merge_block(): jnp.einsum('hqk,khd->hqd', raised.astype(jnp.bfloat16), block_pair[1], pr...  8.08 us
    dot_general x4, matrix products, merge_block(): jnp.einsum('qhd,khd->hqk', queries, block_pair[0], preferred_element_type...  6.46 us
    reshape x2, local copies, waits for them, and re-layouts, on_device(): video_split = video_qkv.reshape(3, video_rows, groups, local_heads, HD)  4.32 us
    all_to_all x1, starting transfers between devices, on_device(): lax.all_to_all(text_split, 'uly', split_axis=2, concat_axis=1, tiled=True)  4.24 us
    all_to_all x1, starting transfers between devices, on_device(): lax.all_to_all(video_split, 'uly', split_axis=2, concat_axis=1, tiled=True)  3.53 us
  transfers between devices with their start and end apart: 5, of which 4 were waited for; matrix products, arithmetic and copies ran while one was open for 4% of the time, Pallas kernels for 0%

commit v1 on v0

v1 whole, which is shorter than its diff:
```python
import functools
import math

import jax
import jax.numpy as jnp
from jax import lax
from jax.experimental import pallas as pl
from jax.experimental.pallas import tpu as pltpu
from jax.sharding import Mesh, PartitionSpec as P

HEADS = 24
HD = 128
VMEM = pltpu.VMEM
ROW_TILE = 8


def up(n, m):
    return -(-n // m) * m


def vspec():
    return pl.BlockSpec(memory_space=VMEM)


def pack_kernel(groups, copies, video, text, q_out, kv_out):
    rows, trows = video.shape[1], text.shape[1]
    width = q_out.shape[2]
    q_pad = q_out.shape[1] - rows - trows
    kv_pad = kv_out.shape[2] - 2 * rows - 2 * trows
    for g in range(groups):
        lanes = slice(g * width, (g + 1) * width)
        q_out[g, :rows, :] = video[0, :, lanes]
        parts = [text[0, :, lanes].astype(jnp.float32), jnp.zeros((q_pad, width), jnp.float32)]
        q_out[g, rows:, :] = jnp.concatenate(parts, axis=0).astype(jnp.bfloat16)
        parts = [
            text[1, :, lanes].astype(jnp.float32),
            text[2, :, lanes].astype(jnp.float32),
            jnp.zeros((kv_pad, width), jnp.float32),
        ]
        tail = jnp.concatenate(parts, axis=0).astype(jnp.bfloat16)
        for c in range(copies):
            kv_out[c, g, :rows, :] = video[1, :, lanes]
            kv_out[c, g, rows : 2 * rows, :] = video[2, :, lanes]
            kv_out[c, g, 2 * rows :, :] = tail


def select_rows(count, tile, first, trows):
    i = lax.broadcasted_iota(jnp.int32, (count * trows, count * tile), 0)
    j = lax.broadcasted_iota(jnp.int32, (count * trows, count * tile), 1)
    want = (i // trows) * tile + first + i % trows
    return jnp.where(j == want, 1.0, 0.0).astype(jnp.bfloat16)


def attend_kernel(rows, trows, per, q_in, kv_in, out):
    sources, qrows, width = q_in.shape
    count, kvrows, _ = kv_in.shape
    heads = width // HD
    total_q = sources * qrows
    tile = kvrows - 2 * rows
    scale = math.log2(math.e) / math.sqrt(HD)
    pick_k = select_rows(per, tile, 0, trows)
    pick_v = select_rows(per, tile, trows, trows)
    nt = (((1,), (1,)), ((), ()))

    def block(h, start):
        lanes = slice(h * HD, (h + 1) * HD)
        span = pl.ds(start, per)
        k = kv_in[span, :rows, lanes].reshape(per * rows, HD)
        v = kv_in[span, rows : 2 * rows, lanes].reshape(per * rows, HD)
        t = kv_in[span, 2 * rows :, lanes].reshape(per * tile, HD)
        kt = jnp.dot(pick_k, t, preferred_element_type=jnp.float32).astype(jnp.bfloat16)
        vt = jnp.dot(pick_v, t, preferred_element_type=jnp.float32).astype(jnp.bfloat16)
        return k, v, kt, vt

    def scores(q, k):
        return lax.dot_general(q, k, nt, preferred_element_type=jnp.float32)

    def weigh(s, best):
        return jnp.exp2((s - best) * scale).astype(jnp.bfloat16)

    def with_ones(v):
        return jnp.concatenate([v, jnp.ones_like(v)], axis=1)

    for h in range(heads):
        lanes = slice(h * HD, (h + 1) * HD)
        q = q_in[:, :, lanes].reshape(total_q, HD)

        def step(i, state):
            k, v, kt, vt = block(h, i * per)
            s, st = scores(q, k), scores(q, kt)
            best = jnp.maximum(jnp.max(s, axis=1, keepdims=True), jnp.max(st, axis=1, keepdims=True))
            if state is not None:
                best = jnp.maximum(best, state[0])
            new = jnp.dot(weigh(s, best), with_ones(v), preferred_element_type=jnp.float32)
            new += jnp.dot(weigh(st, best), with_ones(vt), preferred_element_type=jnp.float32)
            if state is not None:
                new += state[1] * jnp.exp2((state[0] - best) * scale)
            return best, new

        state = step(0, None)
        if count > per:
            state = lax.fori_loop(1, count // per, step, state)
        summed = state[1]
        o = summed[:, :HD] / summed[:, HD:]
        out[:, :, lanes] = o.reshape(sources, qrows, HD).astype(jnp.bfloat16)


def unpack_kernel(o_in, video_gate, text_gate, video_out, text_out):
    rows, trows = video_out.shape[0], text_out.shape[0]
    groups, _, width = o_in.shape
    for g in range(groups):
        lanes = slice(g * width, (g + 1) * width)
        x = o_in[g, :rows, :].astype(jnp.float32)
        video_out[:, lanes] = (x * video_gate[:, lanes]).astype(jnp.bfloat16)
        x = o_in[g, rows:, :].astype(jnp.float32)[:trows]
        text_out[:, lanes] = (x * text_gate[:, lanes]).astype(jnp.bfloat16)


def on_device(video_qkv, text_qkv, video_gate, text_gate):
    halves, planes, uly = lax.axis_size("half"), lax.axis_size("plane"), lax.axis_size("uly")
    groups = planes * uly
    count = halves * groups
    rows, trows = video_qkv.shape[1], text_qkv.shape[1]
    width = HEADS // groups * HD
    q_rows = up(rows + trows, ROW_TILE)
    kv_rows = up(2 * rows + 2 * trows, ROW_TILE)
    bf16 = jnp.bfloat16
    limit = pltpu.CompilerParams(vmem_limit_bytes=56 * 1024 * 1024)
    q_pack, kv_pack = pl.pallas_call(
        functools.partial(pack_kernel, groups, halves),
        out_shape=(
            jax.ShapeDtypeStruct((groups, q_rows, width), bf16),
            jax.ShapeDtypeStruct((halves, groups, kv_rows, width), bf16),
        ),
        in_specs=[vspec()] * 2,
        out_specs=(vspec(), vspec()),
        name="pack",
    )(video_qkv, text_qkv)
    kv = lax.all_to_all(
        kv_pack.reshape(count, kv_rows, width),
        ("half", "plane", "uly"), split_axis=0, concat_axis=0, tiled=True,
    )
    q = lax.all_to_all(q_pack, ("plane", "uly"), split_axis=0, concat_axis=0, tiled=True)
    per = count
    while per * rows > 1024 and per % 2 == 0:
        per //= 2
    o = pl.pallas_call(
        functools.partial(attend_kernel, rows, trows, per),
        out_shape=jax.ShapeDtypeStruct((groups, q_rows, width), bf16),
        in_specs=[vspec()] * 2,
        out_specs=vspec(),
        compiler_params=limit,
        name="attend",
    )(q, kv)
    back = lax.all_to_all(o, ("plane", "uly"), split_axis=0, concat_axis=0, tiled=True)
    return pl.pallas_call(
        unpack_kernel,
        out_shape=(
            jax.ShapeDtypeStruct((rows, HEADS * HD), bf16),
            jax.ShapeDtypeStruct((trows, HEADS * HD), bf16),
        ),
        in_specs=[vspec()] * 3,
        out_specs=(vspec(), vspec()),
        name="unpack",
    )(back, video_gate[None, :], text_gate[None, :])


def solution(mesh):
    req, blk, uly = (mesh.shape[name] for name in ("req", "blk", "uly"))
    planes = max(p for p in range(1, blk + 1) if blk % p == 0 and HEADS % (p * uly) == 0)
    fine = Mesh(
        mesh.devices.reshape(req, blk // planes, planes, uly), ("req", "half", "plane", "uly")
    )
    every = ("req", "half", "plane", "uly")
    in_specs = (P(None, every, None), P(None, every, None), P("req"), P("req"))
    out_specs = (P(every, None), P(every, None))
    return jax.shard_map(
        on_device, mesh=fine, in_specs=in_specs, out_specs=out_specs, check_vma=False
    )
```

time: 150 us -> 82.8 us (0.55)
  waiting for transfers between devices: 92.8 us -> 0 us
  blocking collectives: 0 us -> 71.3 us
  matrix products: 14.5 us -> 0 us
  starting transfers between devices: 14.5 us -> 0 us
  between operations: 14.2 us -> 0.63 us
  Pallas kernels: 0 us -> 10.5 us
  local copies, waits for them, and re-layouts: 7.71 us -> 0 us
  other arithmetic: 4.76 us -> 0 us
    all_to_all x0 -> x3, blocking collectives: none -> 71.3 us  [the longest x1 45 us: on_device(): lax.all_to_all(kv_pack.reshape(count, kv_rows, width), ('half', 'plane',...]
    all_gather x1 -> x0, waiting for transfers between devices: 66 us -> none  [attend(): piece = lax.all_gather(key_pairs, 'blk', axis=1, tiled=True)]
    all_to_all x4 -> x0, waiting for transfers between devices: 26.8 us -> none  [the longest x1 15.7 us: on_device(): lax.all_to_all(video_split, 'uly', split_axis=2, concat_axis=1, tiled=True)]
    dot_general x8 -> x0, matrix products: 14.5 us -> none  [the longest x4 8.08 us: merge_block(): jnp.einsum('hqk,khd->hqd', raised.astype(jnp.bfloat16), block_pair[1], pr...]
    all_to_all x4 -> x0, starting transfers between devices: 14.5 us -> none  [the longest x1 4.24 us: on_device(): lax.all_to_all(text_split, 'uly', split_axis=2, concat_axis=1, tiled=True)]
    pallas_call x0 -> x3, Pallas kernels: none -> 10.5 us  [the longest x1 5.83 us: on_device(): pl.pallas_call(functools.partial(attend_kernel, rows, trows, per), out_sh...]
    reshape x6 -> x0, local copies, waits for them, and re-layouts: 7.21 us -> none  [the longest x2 4.32 us: on_device(): video_split = video_qkv.reshape(3, video_rows, groups, local_heads, HD)]
    convert_element_type x5 -> x0, other arithmetic: 1.89 us -> none  [the longest x1 0.8 us: on_device(): video_out = (video_flat * video_gate[None, :]).astype(jnp.bfloat16)]
  transfers between devices with their start and end apart: 5 -> 0, of which waited for: 4 -> 0; matrix products, arithmetic and copies ran while one was open for 4% -> 0% of each run, Pallas kernels for 0% -> 0%
where the time goes in v1:
time: 82.8 us; the launch traced here: 82.4 us
  blocking collectives  71.3 us (86%)
  Pallas kernels  10.5 us (13%)
    all_to_all x1, blocking collectives, on_device(): lax.all_to_all(kv_pack.reshape(count, kv_rows, width), ('half', 'plane',...  45 us
    all_to_all x1, blocking collectives, on_device(): lax.all_to_all(q_pack, ('plane', 'uly'), split_axis=0, concat_axis=0, til...  13.8 us
    all_to_all x1, blocking collectives, on_device(): lax.all_to_all(o, ('plane', 'uly'), split_axis=0, concat_axis=0, tiled=True)  12.5 us
    pallas_call x1, Pallas kernels, on_device(): pl.pallas_call(functools.partial(attend_kernel, rows, trows, per), out_sh...  5.83 us
    pallas_call x1, Pallas kernels, on_device(): pl.pallas_call(functools.partial(pack_kernel, groups, halves), out_shape=...  2.81 us
    pallas_call x1, Pallas kernels, on_device(): pl.pallas_call(unpack_kernel, out_shape=(jax.ShapeDtypeStruct((rows, HEAD...  1.86 us

profile of v1, /device:TPU:0, one launch (start us, length us, event | category | flops | bytes accessed | tf_op | source)
XLA Modules:
  0.0 82.4 jit_solution(15519313417611482706)
XLA Ops:
  0.6 2.8 %pack.1 = (bf16[8,72,384]{2,1,0:T(8,128)(2,1)}, bf16[2,8,136,384]{3,2,1,0:T(8,128)(2,1)}) custom-call(bf16[3,64,3072]{2,1,0:T(8,128)(2,1)} %video.1, bf16[3,2,3072]{2,1,0:T(2,128)(2,1)} %text.1), custom_call_target="tpu_custom_call" | custom-call | tf_op jit(solution)/shard_map/pack/pallas_call | solution.py:129
  3.4 13.8 %all_to_all.15.q_in = bf16[8,72,384]{2,1,0:T(8,128)(2,1)} all-to-all(bf16[8,72,384]{2,1,0:T(8,128)(2,1)} %get-tuple-element.4), channel_id=1, replica_groups=mesh['req'=2,'half'=2,'plane'=2,'uly'=4] {'plane','uly'}, dimensions={0} | all-to-all | bytes 884736 | tf_op jit(solution)/shard_map/all_to_all | solution.py:143
  17.2 45.0 %all_to_all.16.kv_in = bf16[16,136,384]{2,1,0:T(8,128)(2,1)} all-to-all(bf16[16,136,384]{2,1,0:T(8,128)(2,1)} %bitcast.3), channel_id=1, replica_groups=mesh['req'=2,'half'=2,'plane'=2,'uly'=4] {'half','plane','uly'}, dimensions={0} | all-to-all | bytes 3342336 | tf_op jit(solution)/shard_map/all_to_all | solution.py:139
  62.2 5.8 %attend.1 = bf16[8,72,384]{2,1,0:T(8,128)(2,1)} custom-call(bf16[8,72,384]{2,1,0:T(8,128)(2,1)} %all_to_all.15.q_in, bf16[16,136,384]{2,1,0:T(8,128)(2,1)} %all_to_all.16.kv_in), custom_call_target="tpu_custom_call" | custom-call | tf_op jit(solution)/shard_map/attend/pallas_call | solution.py:147
  68.1 12.5 %all_to_all.17.o_in = bf16[8,72,384]{2,1,0:T(8,128)(2,1)} all-to-all(bf16[8,72,384]{2,1,0:T(8,128)(2,1)} %attend.1), channel_id=1, replica_groups=mesh['req'=2,'half'=2,'plane'=2,'uly'=4] {'plane','uly'}, dimensions={0} | all-to-all | bytes 884736 | tf_op jit(solution)/shard_map/all_to_all | solution.py:155
  80.6 1.9 %unpack.1 = (bf16[64,3072]{1,0:T(8,128)(2,1)}, bf16[2,3072]{1,0:T(2,128)(2,1)}) custom-call(bf16[8,72,384]{2,1,0:T(8,128)(2,1)} %all_to_all.17.o_in, f32[1,3072]{1,0:T(1,128)} %bitcast.4, f32[1,3072]{1,0:T(1,128)} %bitcast.5), custom_call_target="tpu_custom_call" | custom-call | tf_op jit(solution)/shard_map/unpack/pallas_call | solution.py:156

commit v2 on v1

--- a/solution.py
+++ b/solution.py
@@ -114,6 +114,160 @@
         video_out[:, lanes] = (x * video_gate[:, lanes]).astype(jnp.bfloat16)
         x = o_in[g, rows:, :].astype(jnp.float32)[:trows]
         text_out[:, lanes] = (x * text_gate[:, lanes]).astype(jnp.bfloat16)
+
+
+def pack_halves_kernel(groups, me, video, text, own, *cross):
+    rows, trows = video.shape[1], text.shape[1]
+    width = own.shape[2]
+
+    def tail(lanes, kinds, total):
+        parts = [text[n, :, lanes].astype(jnp.float32) for n in kinds]
+        parts.append(jnp.zeros((total - len(kinds) * trows, width), jnp.float32))
+        return jnp.concatenate(parts, axis=0).astype(jnp.bfloat16)
+
+    for i, out in enumerate(cross):
+        lanes = pl.ds(pl.multiple_of(lax.rem(me[0] + i, groups) * width, HD), width)
+        out[:rows, :] = video[1, :, lanes]
+        out[rows : 2 * rows, :] = video[2, :, lanes]
+        out[2 * rows :, :] = tail(lanes, (1, 2), out.shape[0] - 2 * rows)
+    for g in range(groups):
+        lanes = slice(g * width, (g + 1) * width)
+        for n in range(3):
+            own[g, n * rows : (n + 1) * rows, :] = video[n, :, lanes]
+        own[g, 3 * rows :, :] = tail(lanes, (0, 1, 2), own.shape[1] - 3 * rows)
+
+
+def head_queries(own, rows, lanes):
+    tile = own.shape[1] - 3 * rows
+    q = own[:, :rows, lanes].reshape(-1, HD)
+    qt = own[:, 3 * rows :, lanes].reshape(own.shape[0] * tile, HD)
+    return jnp.concatenate([q, qt], axis=0)
+
+
+def dot_nt(a, b):
+    return lax.dot_general(a, b, (((1,), (1,)), ((), ())), preferred_element_type=jnp.float32)
+
+
+def add_keys(q, k, v, kt, vt, state):
+    scale = math.log2(math.e) / math.sqrt(HD)
+    s, st = dot_nt(q, k), dot_nt(q, kt)
+    best = jnp.maximum(jnp.max(s, axis=1, keepdims=True), jnp.max(st, axis=1, keepdims=True))
+    if state is not None:
+        best = jnp.maximum(best, state[0])
+    new = None
+    for score, value in ((s, v), (st, vt)):
+        weights = jnp.exp2((score - best) * scale).astype(jnp.bfloat16)
+        value = jnp.concatenate([value, jnp.ones_like(value)], axis=1)
+        term = jnp.dot(weights, value, preferred_element_type=jnp.float32)
+        new = term if new is None else new + term
+    if state is not None:
+        new += state[1] * jnp.exp2((state[0] - best) * scale)
+    return best, new
+
+
+def pick(pick_rows, t):
+    return jnp.dot(pick_rows, t, preferred_element_type=jnp.float32).astype(jnp.bfloat16)
+
+
+def own_kernel(rows, trows, own, state_out):
+    groups, total, width = own.shape
+    tile = total - 3 * rows
+    pick_k = select_rows(groups, tile, trows, trows)
+    pick_v = select_rows(groups, tile, 2 * trows, trows)
+    for h in range(width // HD):
+        lanes = slice(h * HD, (h + 1) * HD)
+        q = head_queries(own, rows, lanes)
+        k = own[:, rows : 2 * rows, lanes].reshape(groups * rows, HD)
+        v = own[:, 2 * rows : 3 * rows, lanes].reshape(groups * rows, HD)
+        t = own[:, 3 * rows :, lanes].reshape(groups * tile, HD)
+        best, summed = add_keys(q, k, v, pick(pick_k, t), pick(pick_v, t), None)
+        state_out[h, :, : 2 * HD] = summed
+        state_out[h, :, 2 * HD :] = jnp.broadcast_to(best, (best.shape[0], HD))
+
+
+def cross_kernel(rows, trows, own, state_in, *rest):
+    cross, out = rest[:-1], rest[-1]
+    groups, total, width = own.shape
+    tile, cross_tile = total - 3 * rows, cross[0].shape[0] - 2 * rows
+    pick_k = select_rows(groups, cross_tile, 0, trows)
+    pick_v = select_rows(groups, cross_tile, trows, trows)
+    for h in range(width // HD):
+        lanes = slice(h * HD, (h + 1) * HD)
+        q = head_queries(own, rows, lanes)
+        k = jnp.concatenate([c[:rows, lanes] for c in cross], axis=0)
+        v = jnp.concatenate([c[rows : 2 * rows, lanes] for c in cross], axis=0)
+        t = jnp.concatenate([c[2 * rows :, lanes] for c in cross], axis=0)
+        state = (state_in[h, :, 2 * HD : 2 * HD + 1], state_in[h, :, : 2 * HD])
+        _, summed = add_keys(q, k, v, pick(pick_k, t), pick(pick_v, t), state)
+        o = (summed[:, :HD] / summed[:, HD:]).astype(jnp.bfloat16)
+        out[:, :rows, lanes] = o[: groups * rows].reshape(groups, rows, HD)
+        out[:, rows:, lanes] = o[groups * rows :].reshape(groups, tile, HD)
+
+
+def two_halves(video_qkv, text_qkv, video_gate, text_gate):
+    planes, uly = lax.axis_size("plane"), lax.axis_size("uly")
+    groups = planes * uly
+    rows, trows = video_qkv.shape[1], text_qkv.shape[1]
+    width = HEADS // groups * HD
+    own_rows = up(3 * rows + 3 * trows, ROW_TILE)
+    cross_rows = up(2 * rows + 2 * trows, ROW_TILE)
+    queries = groups * (own_rows - 2 * rows)
+    bf16, sds = jnp.bfloat16, jax.ShapeDtypeStruct
+    limit = pltpu.CompilerParams(vmem_limit_bytes=40 * 1024 * 1024)
+    me = lax.axis_index(("plane", "uly")).astype(jnp.int32).reshape(1)
+    own, *cross = pl.pallas_call(
+        functools.partial(pack_halves_kernel, groups),
+        out_shape=(sds((groups, own_rows, width), bf16),)
+        + (sds((cross_rows, width), bf16),) * groups,
+        in_specs=[pl.BlockSpec(memory_space=pltpu.SMEM), vspec(), vspec()],
+        out_specs=(vspec(),) * (1 + groups),
+        name="pack",
+    )(me, video_qkv, text_qkv)
+    landed = []
+    for i, block in enumerate(cross):
+        perm = [
+            (h * groups + g, (1 - h) * groups + (g + i) % groups)
+            for h in range(2)
+            for g in range(groups)
+        ]
+        landed.append(lax.ppermute(block, ("half", "plane", "uly"), perm))
+    own = lax.all_to_all(own, ("plane", "uly"), split_axis=0, concat_axis=0, tiled=True)
+    heads = width // HD
+    flops = 4 * queries * groups * (rows + trows) * width
+    cost = pl.CostEstimate(flops=flops, bytes_accessed=4 << 20, transcendentals=0)
+    state = pl.pallas_call(
+        functools.partial(own_kernel, rows, trows),
+        out_shape=sds((heads, queries, 3 * HD), jnp.float32),
+        in_specs=[vspec()],
+        out_specs=vspec(),
+        compiler_params=limit,
+        cost_estimate=cost,
+        name="own_keys",
+    )(own)
+    o = pl.pallas_call(
+        functools.partial(cross_kernel, rows, trows),
+        out_shape=sds((groups, own_rows - 2 * rows, width), bf16),
+        in_specs=[vspec()] * (2 + groups),
+        out_specs=vspec(),
+        compiler_params=limit,
+        cost_estimate=cost,
+        name="cross_keys",
+    )(own, state, *landed)
+    back = lax.all_to_all(o, ("plane", "uly"), split_axis=0, concat_axis=0, tiled=True)
+    return finish(back, video_gate, text_gate, rows, trows)
+
+
+def finish(back, video_gate, text_gate, rows, trows):
+    return pl.pallas_call(
+        unpack_kernel,
+        out_shape=(
+            jax.ShapeDtypeStruct((rows, HEADS * HD), jnp.bfloat16),
+            jax.ShapeDtypeStruct((trows, HEADS * HD), jnp.bfloat16),
+        ),
+        in_specs=[vspec()] * 3,
+        out_specs=(vspec(), vspec()),
+        name="unpack",
+    )(back, video_gate[None, :], text_gate[None, :])
 
 
 def on_device(video_qkv, text_qkv, video_gate, text_gate):
@@ -153,16 +307,7 @@
         name="attend",
     )(q, kv)
     back = lax.all_to_all(o, ("plane", "uly"), split_axis=0, concat_axis=0, tiled=True)
-    return pl.pallas_call(
-        unpack_kernel,
-        out_shape=(
-            jax.ShapeDtypeStruct((rows, HEADS * HD), bf16),
-            jax.ShapeDtypeStruct((trows, HEADS * HD), bf16),
-        ),
-        in_specs=[vspec()] * 3,
-        out_specs=(vspec(), vspec()),
-        name="unpack",
-    )(back, video_gate[None, :], text_gate[None, :])
+    return finish(back, video_gate, text_gate, rows, trows)
 
 
 def solution(mesh):
@@ -175,5 +320,5 @@
     in_specs = (P(None, every, None), P(None, every, None), P("req"), P("req"))
     out_specs = (P(every, None), P(every, None))
     return jax.shard_map(
-        on_device, mesh=fine, in_specs=in_specs, out_specs=out_specs, check_vma=False
+        two_halves if blk == 2 * planes else on_device, mesh=fine, in_specs=in_specs, out_specs=out_specs, check_vma=False
     )

time: 82.8 us -> 70.3 us (0.85)
  blocking collectives: 71.3 us -> 12.2 us
  waiting for transfers between devices: 0 us -> 28.9 us
  starting transfers between devices: 0 us -> 18.8 us
  Pallas kernels: 10.5 us -> 9.38 us
    all_to_all x3 -> x1, blocking collectives: 71.3 us -> 12.2 us  [two_halves(): lax.all_to_all(o, ('plane', 'uly'), split_axis=0, concat_axis=0, tiled=True)]
    ppermute x0 -> x8, waiting for transfers between devices: none -> 28.8 us  [two_halves(): landed.append(lax.ppermute(block, ('half', 'plane', 'uly'), perm))]
    ppermute x0 -> x8, starting transfers between devices: none -> 13.4 us  [two_halves(): landed.append(lax.ppermute(block, ('half', 'plane', 'uly'), perm))]
    all_to_all x0 -> x1, starting transfers between devices: none -> 5.4 us  [two_halves(): lax.all_to_all(own, ('plane', 'uly'), split_axis=0, concat_axis=0, tiled=...]
    pallas_call x3 -> x4, Pallas kernels: 10.5 us -> 9.38 us  [the longest x1 2.72 us: two_halves(): pl.pallas_call(functools.partial(pack_halves_kernel, groups), out_shape=(...]
  transfers between devices with their start and end apart: 0 -> 9, of which waited for: 0 -> 5; matrix products, arithmetic and copies ran while one was open for 0% -> 0% of each run, Pallas kernels for 0% -> 3%
where the time goes in v2:
time: 70.3 us; the launch traced here: 70 us
  waiting for transfers between devices  28.9 us (41%)
  starting transfers between devices  18.8 us (27%)
  blocking collectives  12.2 us (17%)
  Pallas kernels  9.38 us (13%)
  between operations  0.74 us (1%)
    ppermute x8, waiting for transfers between devices, two_halves(): landed.append(lax.ppermute(block, ('half', 'plane', 'uly'), perm))  28.8 us
    ppermute x8, starting transfers between devices, two_halves(): landed.append(lax.ppermute(block, ('half', 'plane', 'uly'), perm))  13.4 us
    all_to_all x1, blocking collectives, two_halves(): lax.all_to_all(o, ('plane', 'uly'), split_axis=0, concat_axis=0, tiled=True)  12.2 us
    all_to_all x1, starting transfers between devices, two_halves(): lax.all_to_all(own, ('plane', 'uly'), split_axis=0, concat_axis=0, tiled=...  5.4 us
    pallas_call x1, Pallas kernels, two_halves(): pl.pallas_call(functools.partial(pack_halves_kernel, groups), out_shape=(...  2.72 us
    pallas_call x1, Pallas kernels, two_halves(): pl.pallas_call(functools.partial(cross_kernel, rows, trows), out_shape=sd...  2.57 us
    pallas_call x1, Pallas kernels, two_halves(): pl.pallas_call(functools.partial(own_kernel, rows, trows), out_shape=sds(...  2.24 us
    pallas_call x1, Pallas kernels, finish(): pl.pallas_call(unpack_kernel, out_shape=(jax.ShapeDtypeStruct((rows, HEAD...  1.86 us
  transfers between devices with their start and end apart: 9, of which 5 were waited for; matrix products, arithmetic and copies ran while one was open for 0% of the time, Pallas kernels for 3%

profile of v2, /device:TPU:0, one launch (start us, length us, event | category | flops | bytes accessed | tf_op | source)
XLA Modules:
  0.0 70.0 jit_solution(3889004999765532231)
XLA Ops:
  0.6 2.7 %pack.1 = (bf16[8,200,384]{2,1,0:T(8,128)(2,1)}, bf16[136,384]{1,0:T(8,128)(2,1)}, bf16[136,384]{1,0:T(8,128)(2,1)}, bf16[136,384]{1,0:T(8,128)(2,1)}, bf16[136,...) custom-call(s32[1]{0:T(128)} %bitcast.me, ...), custom_call_target="tpu_custom_call" | custom-call | tf_op jit(solution)/shard_map/pack/pallas_call | solution.py:218
  3.4 0.0 copy-start.6
  3.4 0.0 copy-start.5
  3.4 0.0 copy-start.4
  3.4 0.0 copy-start.3
  3.4 0.0 copy-start.2
  3.4 0.0 copy-start.1
  3.4 0.0 copy-start
  3.4 5.4 %all-to-all-start = ((bf16[8,200,384]{2,1,0:T(8,128)(2,1)}), bf16[8,200,384]{2,1,0:T(8,128)(2,1)S(1)}, u32[]{:S(2)}, u32[]{:S(2)}) async-start(bf16[8,200,384]{2,1,0:T(8,128)(2,1)} %get-tuple-element.11), calls=%async_computation | async-start | bytes 2457600 | tf_op jit(solution)/shard_map/all_to_all | solution.py:234
  8.8 0.0 copy-done.7
  8.8 2.7 %collective-permute-start = (bf16[136,384]{1,0:T(8,128)(2,1)S(1)}, bf16[136,384]{1,0:T(8,128)(2,1)S(1)}, u32[]{:S(2)}, u32[]{:S(2)}) collective-permute-start(bf16[136,384]{1,0:T(8,128)(2,1)S(1)} %copy-done.7), channel_id=1, source_target_pairs={{0,8},{1,9},{2,10},{3,11},{4,12},{5,13},{6,14},{7,15},{8,0},{9,1},... | collective-permute-start | bytes 313352 | tf_op jit(solution)/shard_map/ppermute | solution.py:233
  11.5 0.1 collective-permute-start.1
  11.6 3.6 %collective-permute-start.2 = (bf16[136,384]{1,0:T(8,128)(2,1)S(1)}, bf16[136,384]{1,0:T(8,128)(2,1)S(1)}, u32[]{:S(2)}, u32[]{:S(2)}) collective-permute-start(bf16[136,384]{1,0:T(8,128)(2,1)S(1)} %copy-done.5), channel_id=1, source_target_pairs={{0,10},{1,11},{2,12},{3,13},{4,14},{5,15},{6,8},{7,9},{8,2},{9,3},... | collective-permute-start | bytes 313352 | tf_op jit(solution)/shard_map/ppermute | solution.py:233
  15.3 1.2 %collective-permute-start.3 = (bf16[136,384]{1,0:T(8,128)(2,1)S(1)}, bf16[136,384]{1,0:T(8,128)(2,1)S(1)}, u32[]{:S(2)}, u32[]{:S(2)}) collective-permute-start(bf16[136,384]{1,0:T(8,128)(2,1)S(1)} %copy-done.4), channel_id=1, source_target_pairs={{0,11},{1,12},{2,13},{3,14},{4,15},{5,8},{6,9},{7,10},{8,3},{9,4},... | collective-permute-start | bytes 313352 | tf_op jit(solution)/shard_map/ppermute | solution.py:233
  16.5 2.6 %collective-permute-start.4 = (bf16[136,384]{1,0:T(8,128)(2,1)S(1)}, bf16[136,384]{1,0:T(8,128)(2,1)S(1)}, u32[]{:S(2)}, u32[]{:S(2)}) collective-permute-start(bf16[136,384]{1,0:T(8,128)(2,1)S(1)} %copy-done.3), channel_id=1, source_target_pairs={{0,12},{1,13},{2,14},{3,15},{4,8},{5,9},{6,10},{7,11},{8,4},{9,5},... | collective-permute-start | bytes 313352 | tf_op jit(solution)/shard_map/ppermute | solution.py:233
  19.1 6.5 %collective-permute-done.rest_0_ = bf16[136,384]{1,0:T(8,128)(2,1)S(1)} collective-permute-done((bf16[136,384]{1,0:T(8,128)(2,1)S(1)}, bf16[136,384]{1,0:T(8,128)(2,1)S(1)}, u32[]{:S(2)}, u32[]{:S(2)}) %collective-permute-start) | collective-permute-done | bytes 104480 | tf_op jit(solution)/shard_map/ppermute | solution.py:233
  25.6 2.6 %collective-permute-start.5 = (bf16[136,384]{1,0:T(8,128)(2,1)S(1)}, bf16[136,384]{1,0:T(8,128)(2,1)S(1)}, u32[]{:S(2)}, u32[]{:S(2)}) collective-permute-start(bf16[136,384]{1,0:T(8,128)(2,1)S(1)} %copy-done.2), channel_id=1, source_target_pairs={{0,13},{1,14},{2,15},{3,8},{4,9},{5,10},{6,11},{7,12},{8,5},{9,6},... | collective-permute-start | bytes 313352 | tf_op jit(solution)/shard_map/ppermute | solution.py:233
  28.2 6.7 %collective-permute-done.1.rest_1_ = bf16[136,384]{1,0:T(8,128)(2,1)S(1)} collective-permute-done((bf16[136,384]{1,0:T(8,128)(2,1)S(1)}, bf16[136,384]{1,0:T(8,128)(2,1)S(1)}, u32[]{:S(2)}, u32[]{:S(2)}) %collective-permute-start.1) | collective-permute-done | bytes 104480 | tf_op jit(solution)/shard_map/ppermute | solution.py:233
  34.9 0.6 collective-permute-start.6
  35.6 2.7 %collective-permute-done.2.rest_2_ = bf16[136,384]{1,0:T(8,128)(2,1)S(1)} collective-permute-done((bf16[136,384]{1,0:T(8,128)(2,1)S(1)}, bf16[136,384]{1,0:T(8,128)(2,1)S(1)}, u32[]{:S(2)}, u32[]{:S(2)}) %collective-permute-start.2) | collective-permute-done | bytes 104480 | tf_op jit(solution)/shard_map/ppermute | solution.py:233
  38.3 0.0 copy-done
  38.3 0.0 collective-permute-start.7
  38.3 0.0 all-to-all-done.own
  38.3 2.2 %own_keys.1.state_in = f32[3,576,384]{2,1,0:T(8,128)S(1)} custom-call(bf16[8,200,384]{2,1,0:T(8,128)(2,1)S(1)} %all-to-all-done.own), custom_call_target="tpu_custom_call" | custom-call | flops 467140608 | bytes 4194304 | tf_op jit(solution)/shard_map/own_keys/pallas_call | solution.py:238
  40.6 0.0 collective-permute-done.3.rest_3_
  40.6 0.0 collective-permute-done.4.rest_4_
  40.6 10.4 %collective-permute-done.5.rest_5_ = bf16[136,384]{1,0:T(8,128)(2,1)S(1)} collective-permute-done((bf16[136,384]{1,0:T(8,128)(2,1)S(1)}, bf16[136,384]{1,0:T(8,128)(2,1)S(1)}, u32[]{:S(2)}, u32[]{:S(2)}) %collective-permute-start.5) | collective-permute-done | bytes 104480 | tf_op jit(solution)/shard_map/ppermute | solution.py:233
  51.0 2.4 %collective-permute-done.6.rest_6_ = bf16[136,384]{1,0:T(8,128)(2,1)S(1)} collective-permute-done((bf16[136,384]{1,0:T(8,128)(2,1)S(1)}, bf16[136,384]{1,0:T(8,128)(2,1)S(1)}, u32[]{:S(2)}, u32[]{:S(2)}) %collective-permute-start.6) | collective-permute-done | bytes 104480 | tf_op jit(solution)/shard_map/ppermute | solution.py:233
  53.4 0.0 collective-permute-done.7.rest_7_
  53.4 2.6 %cross_keys.1 = bf16[8,72,384]{2,1,0:T(8,128)(2,1)S(1)} custom-call(bf16[8,200,384]{2,1,0:T(8,128)(2,1)S(1)} %all-to-all-done.own, f32[3,576,384]{2,1,0:T(8,128)S(1)} %own_keys.1.state_in, bf16[136,384]{1,0:T(8,128)(2,1)S(1)} %collective-permute-done.rest_0_, bf16[136,384]{1,0:T(8,128)(2,1)S(1)} %collective-permute-done.1.rest_1_, ...), custom_call_target="tpu_custom_call" | custom-call | flops 467140608 | bytes 4194304 | tf_op jit(solution)/shard_map/cross_keys/pallas_call | solution.py:247
  56.0 12.2 %all_to_all.10.o_in = bf16[8,72,384]{2,1,0:T(8,128)(2,1)} all-to-all(bf16[8,72,384]{2,1,0:T(8,128)(2,1)S(1)} %cross_keys.1), channel_id=1, replica_groups=mesh['req'=2,'half'=2,'plane'=2,'uly'=4] {'plane','uly'}, dimensions={0} | all-to-all | bytes 884736 | tf_op jit(solution)/shard_map/all_to_all | solution.py:256
  68.2 1.9 %unpack.1 = (bf16[64,3072]{1,0:T(8,128)(2,1)}, bf16[2,3072]{1,0:T(2,128)(2,1)}) custom-call(bf16[8,72,384]{2,1,0:T(8,128)(2,1)} %all_to_all.10.o_in, f32[1,3072]{1,0:T(1,128)} %bitcast.3, f32[1,3072]{1,0:T(1,128)} %bitcast.4), custom_call_target="tpu_custom_call" | custom-call | tf_op jit(solution)/shard_map/unpack/pallas_call | solution.py:261
  (7 shorter events, 0.0 us)
Async XLA Ops:
  3.4 5.5 %copy-start.7 = (bf16[136,384]{1,0:T(8,128)(2,1)S(1)}, bf16[136,384]{1,0:T(8,128)(2,1)}, u32[]{:S(2)}) copy-start(bf16[136,384]{1,0:T(8,128)(2,1)} %get-tuple-element.12) | copy-start | bytes 313348
  3.4 8.1 %copy-start.6 = (bf16[136,384]{1,0:T(8,128)(2,1)S(1)}, bf16[136,384]{1,0:T(8,128)(2,1)}, u32[]{:S(2)}) copy-start(bf16[136,384]{1,0:T(8,128)(2,1)} %get-tuple-element.13) | copy-start | bytes 313348
  3.4 8.2 %copy-start.5 = (bf16[136,384]{1,0:T(8,128)(2,1)S(1)}, bf16[136,384]{1,0:T(8,128)(2,1)}, u32[]{:S(2)}) copy-start(bf16[136,384]{1,0:T(8,128)(2,1)} %get-tuple-element.14) | copy-start | bytes 313348
  3.4 11.9 %copy-start.4 = (bf16[136,384]{1,0:T(8,128)(2,1)S(1)}, bf16[136,384]{1,0:T(8,128)(2,1)}, u32[]{:S(2)}) copy-start(bf16[136,384]{1,0:T(8,128)(2,1)} %get-tuple-element.15) | copy-start | bytes 313348
  3.4 13.1 %copy-start.3 = (bf16[136,384]{1,0:T(8,128)(2,1)S(1)}, bf16[136,384]{1,0:T(8,128)(2,1)}, u32[]{:S(2)}) copy-start(bf16[136,384]{1,0:T(8,128)(2,1)} %get-tuple-element.16) | copy-start | bytes 313348
  3.4 22.2 %copy-start.2 = (bf16[136,384]{1,0:T(8,128)(2,1)S(1)}, bf16[136,384]{1,0:T(8,128)(2,1)}, u32[]{:S(2)}) copy-start(bf16[136,384]{1,0:T(8,128)(2,1)} %get-tuple-element.17) | copy-start | bytes 313348
  3.4 31.5 %copy-start.1 = (bf16[136,384]{1,0:T(8,128)(2,1)S(1)}, bf16[136,384]{1,0:T(8,128)(2,1)}, u32[]{:S(2)}) copy-start(bf16[136,384]{1,0:T(8,128)(2,1)} %get-tuple-element.18) | copy-start | bytes 313348
  3.4 34.9 %copy-start = (bf16[136,384]{1,0:T(8,128)(2,1)S(1)}, bf16[136,384]{1,0:T(8,128)(2,1)}, u32[]{:S(2)}) copy-start(bf16[136,384]{1,0:T(8,128)(2,1)} %get-tuple-element.19) | copy-start | bytes 313348
  3.4 34.9 %all-to-all-start = ((bf16[8,200,384]{2,1,0:T(8,128)(2,1)}), bf16[8,200,384]{2,1,0:T(8,128)(2,1)S(1)}, u32[]{:S(2)}, u32[]{:S(2)}) async-start(bf16[8,200,384]{2,1,0:T(8,128)(2,1)} %get-tuple-element.11), calls=%async_computation | async-start | bytes 2457600 | tf_op jit(solution)/shard_map/all_to_all | solution.py:234
  8.8 16.8 %collective-permute-start = (bf16[136,384]{1,0:T(8,128)(2,1)S(1)}, bf16[136,384]{1,0:T(8,128)(2,1)S(1)}, u32[]{:S(2)}, u32[]{:S(2)}) collective-permute-start(bf16[136,384]{1,0:T(8,128)(2,1)S(1)} %copy-done.7), channel_id=1, source_target_pairs={{0,8},{1,9},{2,10},{3,11},{4,12},{5,13},{6,14},{7,15},{8,0},{9,1},... | collective-permute-start | bytes 313352 | tf_op jit(solution)/shard_map/ppermute | solution.py:233
  11.5 23.4 %collective-permute-start.1 = (bf16[136,384]{1,0:T(8,128)(2,1)S(1)}, bf16[136,384]{1,0:T(8,128)(2,1)S(1)}, u32[]{:S(2)}, u32[]{:S(2)}) collective-permute-start(bf16[136,384]{1,0:T(8,128)(2,1)S(1)} %copy-done.6), channel_id=1, source_target_pairs={{0,9},{1,10},{2,11},{3,12},{4,13},{5,14},{6,15},{7,8},{8,1},{9,2},... | collective-permute-start | bytes 313352 | tf_op jit(solution)/shard_map/ppermute | solution.py:233
  11.6 26.7 %collective-permute-start.2 = (bf16[136,384]{1,0:T(8,128)(2,1)S(1)}, bf16[136,384]{1,0:T(8,128)(2,1)S(1)}, u32[]{:S(2)}, u32[]{:S(2)}) collective-permute-start(bf16[136,384]{1,0:T(8,128)(2,1)S(1)} %copy-done.5), channel_id=1, source_target_pairs={{0,10},{1,11},{2,12},{3,13},{4,14},{5,15},{6,8},{7,9},{8,2},{9,3},... | collective-permute-start | bytes 313352 | tf_op jit(solution)/shard_map/ppermute | solution.py:233
  15.3 25.3 %collective-permute-start.3 = (bf16[136,384]{1,0:T(8,128)(2,1)S(1)}, bf16[136,384]{1,0:T(8,128)(2,1)S(1)}, u32[]{:S(2)}, u32[]{:S(2)}) collective-permute-start(bf16[136,384]{1,0:T(8,128)(2,1)S(1)} %copy-done.4), channel_id=1, source_target_pairs={{0,11},{1,12},{2,13},{3,14},{4,15},{5,8},{6,9},{7,10},{8,3},{9,4},... | collective-permute-start | bytes 313352 | tf_op jit(solution)/shard_map/ppermute | solution.py:233
  16.5 24.1 %collective-permute-start.4 = (bf16[136,384]{1,0:T(8,128)(2,1)S(1)}, bf16[136,384]{1,0:T(8,128)(2,1)S(1)}, u32[]{:S(2)}, u32[]{:S(2)}) collective-permute-start(bf16[136,384]{1,0:T(8,128)(2,1)S(1)} %copy-done.3), channel_id=1, source_target_pairs={{0,12},{1,13},{2,14},{3,15},{4,8},{5,9},{6,10},{7,11},{8,4},{9,5},... | collective-permute-start | bytes 313352 | tf_op jit(solution)/shard_map/ppermute | solution.py:233
  25.6 25.4 %collective-permute-start.5 = (bf16[136,384]{1,0:T(8,128)(2,1)S(1)}, bf16[136,384]{1,0:T(8,128)(2,1)S(1)}, u32[]{:S(2)}, u32[]{:S(2)}) collective-permute-start(bf16[136,384]{1,0:T(8,128)(2,1)S(1)} %copy-done.2), channel_id=1, source_target_pairs={{0,13},{1,14},{2,15},{3,8},{4,9},{5,10},{6,11},{7,12},{8,5},{9,6},... | collective-permute-start | bytes 313352 | tf_op jit(solution)/shard_map/ppermute | solution.py:233
  34.9 18.5 %collective-permute-start.6 = (bf16[136,384]{1,0:T(8,128)(2,1)S(1)}, bf16[136,384]{1,0:T(8,128)(2,1)S(1)}, u32[]{:S(2)}, u32[]{:S(2)}) collective-permute-start(bf16[136,384]{1,0:T(8,128)(2,1)S(1)} %copy-done.1), channel_id=1, source_target_pairs={{0,14},{1,15},{2,8},{3,9},{4,10},{5,11},{6,12},{7,13},{8,6},{9,7},... | collective-permute-start | bytes 313352 | tf_op jit(solution)/shard_map/ppermute | solution.py:233
  38.3 15.1 %collective-permute-start.7 = (bf16[136,384]{1,0:T(8,128)(2,1)S(1)}, bf16[136,384]{1,0:T(8,128)(2,1)S(1)}, u32[]{:S(2)}, u32[]{:S(2)}) collective-permute-start(bf16[136,384]{1,0:T(8,128)(2,1)S(1)} %copy-done), channel_id=1, source_target_pairs={{0,15},{1,8},{2,9},{3,10},{4,11},{5,12},{6,13},{7,14},{8,7},{9,0},... | collective-permute-start | bytes 313352 | tf_op jit(solution)/shard_map/ppermute | solution.py:233

commit v3 on v2

--- a/solution.py
+++ b/solution.py
@@ -116,25 +116,44 @@
         text_out[:, lanes] = (x * text_gate[:, lanes]).astype(jnp.bfloat16)
 
 
-def pack_halves_kernel(groups, me, video, text, own, *cross):
-    rows, trows = video.shape[1], text.shape[1]
-    width = own.shape[2]
-
-    def tail(lanes, kinds, total):
-        parts = [text[n, :, lanes].astype(jnp.float32) for n in kinds]
-        parts.append(jnp.zeros((total - len(kinds) * trows, width), jnp.float32))
-        return jnp.concatenate(parts, axis=0).astype(jnp.bfloat16)
-
+def tail_rows(text, lanes, kinds, total):
+    trows = text.shape[1]
+    parts = [text[n, :, lanes].astype(jnp.float32) for n in kinds]
+    parts.append(jnp.zeros((total - len(kinds) * trows, parts[0].shape[1]), jnp.float32))
+    return jnp.concatenate(parts, axis=0).astype(jnp.bfloat16)
+
+
+def pack_cross_kernel(rows, me, video, text, *rest):
+    cross, sems = rest[:-1], rest[-1]
+    copies = []
     for i, out in enumerate(cross):
-        lanes = pl.ds(pl.multiple_of(lax.rem(me[0] + i, groups) * width, HD), width)
-        out[:rows, :] = video[1, :, lanes]
-        out[rows : 2 * rows, :] = video[2, :, lanes]
-        out[2 * rows :, :] = tail(lanes, (1, 2), out.shape[0] - 2 * rows)
+        width = out.shape[1]
+        lanes = pl.ds(pl.multiple_of((me[0] ^ i) * width, HD), width)
+        for n in range(2):
+            copy = pltpu.make_async_copy(
+                video.at[1 + n, :, lanes], out.at[n * rows : (n + 1) * rows, :], sems.at[i, n]
+            )
+            copy.start()
+            copies.append(copy)
+        out[2 * rows :, :] = tail_rows(text, lanes, (1, 2), out.shape[0] - 2 * rows)
+    for copy in copies:
+        copy.wait()
+
+
+def pack_own_kernel(rows, video, text, own, sems):
+    groups, total, width = own.shape
+    copies = []
     for g in range(groups):
         lanes = slice(g * width, (g + 1) * width)
         for n in range(3):
-            own[g, n * rows : (n + 1) * rows, :] = video[n, :, lanes]
-        own[g, 3 * rows :, :] = tail(lanes, (0, 1, 2), own.shape[1] - 3 * rows)
+            copy = pltpu.make_async_copy(
+                video.at[n, :, lanes], own.at[g, n * rows : (n + 1) * rows, :], sems.at[g, n]
+            )
+            copy.start()
+            copies.append(copy)
+        own[g, 3 * rows :, :] = tail_rows(text, lanes, (0, 1, 2), total - 3 * rows)
+    for copy in copies:
+        copy.wait()
 
 
 def head_queries(own, rows, lanes):
@@ -215,18 +234,30 @@
     bf16, sds = jnp.bfloat16, jax.ShapeDtypeStruct
     limit = pltpu.CompilerParams(vmem_limit_bytes=40 * 1024 * 1024)
     me = lax.axis_index(("plane", "uly")).astype(jnp.int32).reshape(1)
-    own, *cross = pl.pallas_call(
-        functools.partial(pack_halves_kernel, groups),
-        out_shape=(sds((groups, own_rows, width), bf16),)
-        + (sds((cross_rows, width), bf16),) * groups,
-        in_specs=[pl.BlockSpec(memory_space=pltpu.SMEM), vspec(), vspec()],
-        out_specs=(vspec(),) * (1 + groups),
-        name="pack",
+    smem, hbm = pl.BlockSpec(memory_space=pltpu.SMEM), pl.BlockSpec(memory_space=pl.ANY)
+    small = pltpu.CompilerParams(vmem_limit_bytes=8 * 1024 * 1024)
+    cross = pl.pallas_call(
+        functools.partial(pack_cross_kernel, rows),
+        out_shape=(sds((cross_rows, width), bf16),) * groups,
+        in_specs=[smem, hbm, vspec()],
+        out_specs=(vspec(),) * groups,
+        scratch_shapes=[pltpu.SemaphoreType.DMA((groups, 2))],
+        compiler_params=small,
+        name="pack_cross",
     )(me, video_qkv, text_qkv)
+    own = pl.pallas_call(
+        functools.partial(pack_own_kernel, rows),
+        out_shape=sds((groups, own_rows, width), bf16),
+        in_specs=[hbm, vspec()],
+        out_specs=vspec(),
+        scratch_shapes=[pltpu.SemaphoreType.DMA((groups, 3))],
+        compiler_params=small,
+        name="pack_own",
+    )(video_qkv, text_qkv)
     landed = []
     for i, block in enumerate(cross):
         perm = [
-            (h * groups + g, (1 - h) * groups + (g + i) % groups)
+            (h * groups + g, (1 - h) * groups + (g ^ i))
             for h in range(2)
             for g in range(groups)
         ]
@@ -266,6 +297,7 @@
         ),
         in_specs=[vspec()] * 3,
         out_specs=(vspec(), vspec()),
+        compiler_params=pltpu.CompilerParams(vmem_limit_bytes=8 * 1024 * 1024),
         name="unpack",
     )(back, video_gate[None, :], text_gate[None, :])
 
@@ -319,6 +351,8 @@
     every = ("req", "half", "plane", "uly")
     in_specs = (P(None, every, None), P(None, every, None), P("req"), P("req"))
     out_specs = (P(every, None), P(every, None))
+    split = blk == 2 * planes and (planes * uly) & (planes * uly - 1) == 0
     return jax.shard_map(
-        two_halves if blk == 2 * planes else on_device, mesh=fine, in_specs=in_specs, out_specs=out_specs, check_vma=False
+        two_halves if split else on_device,
+        mesh=fine, in_specs=in_specs, out_specs=out_specs, check_vma=False,
     )

time: 70.3 us -> 67.4 us (0.959)
  waiting for transfers between devices: 28.9 us -> 15.6 us
  starting transfers between devices: 18.8 us -> 23.9 us
  blocking collectives: 12.2 us -> 17.2 us
  local copies, waits for them, and re-layouts: 0.03 us -> 2.06 us
  Pallas kernels: 9.38 us -> 7.56 us
    ppermute x8, waiting for transfers between devices: 28.8 us -> 15.3 us  [two_halves(): landed.append(lax.ppermute(block, ('half', 'plane', 'uly'), perm))]
    all_to_all x1, blocking collectives: 12.2 us -> 17.2 us  [two_halves(): lax.all_to_all(o, ('plane', 'uly'), split_axis=0, concat_axis=0, tiled=True)]
    ppermute x8, starting transfers between devices: 13.4 us -> 18.5 us  [two_halves(): landed.append(lax.ppermute(block, ('half', 'plane', 'uly'), perm))]
    unnamed x16 -> x12, local copies, waits for them, and re-layouts: 0.03 us -> 2.06 us
    pallas_call x1, Pallas kernels: 1.86 us -> 0.83 us  [finish(): pl.pallas_call(unpack_kernel, out_shape=(jax.ShapeDtypeStruct((rows, HEAD...]
    pallas_call x1 -> x2, Pallas kernels: 2.72 us -> 1.92 us  [the longest x1 1.57 us: two_halves(): pl.pallas_call(functools.partial(pack_own_kernel, rows), out_shape=sds((g...]
  transfers between devices with their start and end apart: 9 -> 9, of which waited for: 5 -> 6; matrix products, arithmetic and copies ran while one was open for 0% -> 0% of each run, Pallas kernels for 3% -> 4%
where the time goes in v3:
time: 67.4 us; the launch traced here: 67.1 us
  starting transfers between devices  23.9 us (35%)
  blocking collectives  17.2 us (26%)
  waiting for transfers between devices  15.6 us (23%)
  Pallas kernels  7.56 us (11%)
  local copies, waits for them, and re-layouts  2.06 us (3%)
  between operations  0.72 us (1%)
    ppermute x8, starting transfers between devices, two_halves(): landed.append(lax.ppermute(block, ('half', 'plane', 'uly'), perm))  18.5 us
    all_to_all x1, blocking collectives, two_halves(): lax.all_to_all(o, ('plane', 'uly'), split_axis=0, concat_axis=0, tiled=True)  17.2 us
    ppermute x8, waiting for transfers between devices, two_halves(): landed.append(lax.ppermute(block, ('half', 'plane', 'uly'), perm))  15.3 us
    all_to_all x1, starting transfers between devices, two_halves(): lax.all_to_all(own, ('plane', 'uly'), split_axis=0, concat_axis=0, tiled=...  5.4 us
    pallas_call x1, Pallas kernels, two_halves(): pl.pallas_call(functools.partial(cross_kernel, rows, trows), out_shape=sd...  2.57 us
    pallas_call x1, Pallas kernels, two_halves(): pl.pallas_call(functools.partial(own_kernel, rows, trows), out_shape=sds(...  2.24 us
    unnamed x12, local copies, waits for them, and re-layouts  2.06 us
    pallas_call x1, Pallas kernels, two_halves(): pl.pallas_call(functools.partial(pack_own_kernel, rows), out_shape=sds((g...  1.57 us
  transfers between devices with their start and end apart: 9, of which 6 were waited for; matrix products, arithmetic and copies ran while one was open for 0% of the time, Pallas kernels for 4%

profile of v3, /device:TPU:0, one launch (start us, length us, event | category | flops | bytes accessed | tf_op | source)
XLA Modules:
  0.0 67.1 jit_solution(8423692636134046599)
XLA Ops:
  0.6 0.0 copy-start
  0.6 1.3 %copy-done = bf16[3,64,3072]{2,1,0:T(8,128)(2,1)S(1)} copy-done((bf16[3,64,3072]{2,1,0:T(8,128)(2,1)S(1)}, bf16[3,64,3072]{2,1,0:T(8,128)(2,1)}, u32[]{:S(2)}) %copy-start) | copy-done | bytes 1179672
  1.9 0.8 %copy-done.2 = bf16[3,2,3072]{2,1,0:T(2,128)(2,1)S(1)} copy-done((bf16[3,2,3072]{2,1,0:T(2,128)(2,1)S(1)}, bf16[3,2,3072]{2,1,0:T(2,128)(2,1)}, u32[]{:S(2)}) %copy-start.2) | copy-done | bytes 36888
  2.7 1.6 %pack_own.1 = bf16[8,200,384]{2,1,0:T(8,128)(2,1)} custom-call(bf16[3,64,3072]{2,1,0:T(8,128)(2,1)S(1)} %copy-done, bf16[3,2,3072]{2,1,0:T(2,128)(2,1)S(1)} %copy-done.2), custom_call_target="tpu_custom_call" | custom-call | tf_op jit(solution)/shard_map/pack_own/pallas_call | solution.py:248
  4.2 0.0 copy-start.1
  4.3 0.0 copy-start.3
  4.3 5.4 %all-to-all-start = ((bf16[8,200,384]{2,1,0:T(8,128)(2,1)}), bf16[8,200,384]{2,1,0:T(8,128)(2,1)S(1)}, u32[]{:S(2)}, u32[]{:S(2)}) async-start(bf16[8,200,384]{2,1,0:T(8,128)(2,1)} %pack_own.1), calls=%async_computation | async-start | bytes 2457600 | tf_op jit(solution)/shard_map/all_to_all | solution.py:265
  9.7 0.0 copy-done.1
  9.7 0.4 pack_cross.1
  10.0 2.7 %collective-permute-start = (bf16[136,384]{1,0:T(8,128)(2,1)S(1)}, bf16[136,384]{1,0:T(8,128)(2,1)S(1)}, u32[]{:S(2)}, u32[]{:S(2)}) collective-permute-start(bf16[136,384]{1,0:T(8,128)(2,1)S(1)} %get-tuple-element.10), channel_id=1, source_target_pairs={{0,8},{1,9},{2,10},{3,11},{4,12},{5,13},{6,14},{7,15},{8,0},{9,1},... | collective-permute-start | bytes 313352 | tf_op jit(solution)/shard_map/ppermute | solution.py:264
  12.7 0.2 collective-permute-start.1
  12.9 3.6 %collective-permute-start.2 = (bf16[136,384]{1,0:T(8,128)(2,1)S(1)}, bf16[136,384]{1,0:T(8,128)(2,1)S(1)}, u32[]{:S(2)}, u32[]{:S(2)}) collective-permute-start(bf16[136,384]{1,0:T(8,128)(2,1)S(1)} %get-tuple-element.12), channel_id=1, source_target_pairs={{0,10},{1,11},{2,8},{3,9},{4,14},{5,15},{6,12},{7,13},{8,2},{9,3},... | collective-permute-start | bytes 313352 | tf_op jit(solution)/shard_map/ppermute | solution.py:264
  16.5 0.3 collective-permute-start.3
  16.8 3.5 %collective-permute-start.4 = (bf16[136,384]{1,0:T(8,128)(2,1)S(1)}, bf16[136,384]{1,0:T(8,128)(2,1)S(1)}, u32[]{:S(2)}, u32[]{:S(2)}) collective-permute-start(bf16[136,384]{1,0:T(8,128)(2,1)S(1)} %get-tuple-element.14), channel_id=1, source_target_pairs={{0,12},{1,13},{2,14},{3,15},{4,8},{5,9},{6,10},{7,11},{8,4},{9,5},... | collective-permute-start | bytes 313352 | tf_op jit(solution)/shard_map/ppermute | solution.py:264
  20.3 6.1 %collective-permute-done.rest_0_ = bf16[136,384]{1,0:T(8,128)(2,1)S(1)} collective-permute-done((bf16[136,384]{1,0:T(8,128)(2,1)S(1)}, bf16[136,384]{1,0:T(8,128)(2,1)S(1)}, u32[]{:S(2)}, u32[]{:S(2)}) %collective-permute-start) | collective-permute-done | bytes 104480 | tf_op jit(solution)/shard_map/ppermute | solution.py:264
  26.5 2.6 %collective-permute-start.5 = (bf16[136,384]{1,0:T(8,128)(2,1)S(1)}, bf16[136,384]{1,0:T(8,128)(2,1)S(1)}, u32[]{:S(2)}, u32[]{:S(2)}) collective-permute-start(bf16[136,384]{1,0:T(8,128)(2,1)S(1)} %get-tuple-element.15), channel_id=1, source_target_pairs={{0,13},{1,12},{2,15},{3,14},{4,9},{5,8},{6,11},{7,10},{8,5},{9,4},... | collective-permute-start | bytes 313352 | tf_op jit(solution)/shard_map/ppermute | solution.py:264
  29.0 0.0 collective-permute-done.1.rest_1_
  29.0 4.6 %collective-permute-start.6 = (bf16[136,384]{1,0:T(8,128)(2,1)S(1)}, bf16[136,384]{1,0:T(8,128)(2,1)S(1)}, u32[]{:S(2)}, u32[]{:S(2)}) collective-permute-start(bf16[136,384]{1,0:T(8,128)(2,1)S(1)} %get-tuple-element.16), channel_id=1, source_target_pairs={{0,14},{1,15},{2,12},{3,13},{4,10},{5,11},{6,8},{7,9},{8,6},{9,7},... | collective-permute-start | bytes 313352 | tf_op jit(solution)/shard_map/ppermute | solution.py:264
  33.6 0.0 collective-permute-done.2.rest_2_
  33.6 1.0 %collective-permute-start.7 = (bf16[136,384]{1,0:T(8,128)(2,1)S(1)}, bf16[136,384]{1,0:T(8,128)(2,1)S(1)}, u32[]{:S(2)}, u32[]{:S(2)}) collective-permute-start(bf16[136,384]{1,0:T(8,128)(2,1)S(1)} %get-tuple-element.17), channel_id=1, source_target_pairs={{0,15},{1,14},{2,13},{3,12},{4,11},{5,10},{6,9},{7,8},{8,7},{9,6},... | collective-permute-start | bytes 313352 | tf_op jit(solution)/shard_map/ppermute | solution.py:264
  34.6 0.4 all-to-all-done.own
  35.0 2.2 %own_keys.1.state_in = f32[3,576,384]{2,1,0:T(8,128)S(1)} custom-call(bf16[8,200,384]{2,1,0:T(8,128)(2,1)S(1)} %all-to-all-done.own), custom_call_target="tpu_custom_call" | custom-call | flops 467140608 | bytes 4194304 | tf_op jit(solution)/shard_map/own_keys/pallas_call | solution.py:269
  37.2 0.0 copy-start.4
  37.2 0.0 copy-start.5
  37.2 0.0 collective-permute-done.3.rest_3_
  37.3 2.7 %collective-permute-done.4.rest_4_ = bf16[136,384]{1,0:T(8,128)(2,1)S(1)} collective-permute-done((bf16[136,384]{1,0:T(8,128)(2,1)S(1)}, bf16[136,384]{1,0:T(8,128)(2,1)S(1)}, u32[]{:S(2)}, u32[]{:S(2)}) %collective-permute-start.4) | collective-permute-done | bytes 104480 | tf_op jit(solution)/shard_map/ppermute | solution.py:264
  40.0 1.1 %collective-permute-done.5.rest_5_ = bf16[136,384]{1,0:T(8,128)(2,1)S(1)} collective-permute-done((bf16[136,384]{1,0:T(8,128)(2,1)S(1)}, bf16[136,384]{1,0:T(8,128)(2,1)S(1)}, u32[]{:S(2)}, u32[]{:S(2)}) %collective-permute-start.5) | collective-permute-done | bytes 104480 | tf_op jit(solution)/shard_map/ppermute | solution.py:264
  41.1 4.3 %collective-permute-done.6.rest_6_ = bf16[136,384]{1,0:T(8,128)(2,1)S(1)} collective-permute-done((bf16[136,384]{1,0:T(8,128)(2,1)S(1)}, bf16[136,384]{1,0:T(8,128)(2,1)S(1)}, u32[]{:S(2)}, u32[]{:S(2)}) %collective-permute-start.6) | collective-permute-done | bytes 104480 | tf_op jit(solution)/shard_map/ppermute | solution.py:264
  45.3 1.1 %collective-permute-done.7.rest_7_ = bf16[136,384]{1,0:T(8,128)(2,1)S(1)} collective-permute-done((bf16[136,384]{1,0:T(8,128)(2,1)S(1)}, bf16[136,384]{1,0:T(8,128)(2,1)S(1)}, u32[]{:S(2)}, u32[]{:S(2)}) %collective-permute-start.7) | collective-permute-done | bytes 104480 | tf_op jit(solution)/shard_map/ppermute | solution.py:264
  46.4 2.6 %cross_keys.1 = bf16[8,72,384]{2,1,0:T(8,128)(2,1)S(1)} custom-call(bf16[8,200,384]{2,1,0:T(8,128)(2,1)S(1)} %all-to-all-done.own, f32[3,576,384]{2,1,0:T(8,128)S(1)} %own_keys.1.state_in, bf16[136,384]{1,0:T(8,128)(2,1)S(1)} %collective-permute-done.rest_0_, bf16[136,384]{1,0:T(8,128)(2,1)S(1)} %collective-permute-done.1.rest_1_, ...), custom_call_target="tpu_custom_call" | custom-call | flops 467140608 | bytes 4194304 | tf_op jit(solution)/shard_map/cross_keys/pallas_call | solution.py:278
  49.0 17.2 %all_to_all.10.o_in = bf16[8,72,384]{2,1,0:T(8,128)(2,1)S(1)} all-to-all(bf16[8,72,384]{2,1,0:T(8,128)(2,1)S(1)} %cross_keys.1), channel_id=1, replica_groups=mesh['req'=2,'half'=2,'plane'=2,'uly'=4] {'plane','uly'}, dimensions={0} | all-to-all | bytes 884736 | tf_op jit(solution)/shard_map/all_to_all | solution.py:287
  66.2 0.8 %unpack.1 = (bf16[64,3072]{1,0:T(8,128)(2,1)}, bf16[2,3072]{1,0:T(2,128)(2,1)}) custom-call(bf16[8,72,384]{2,1,0:T(8,128)(2,1)S(1)} %all_to_all.10.o_in, f32[1,3072]{1,0:T(1,128)S(1)} %bitcast.3, f32[1,3072]{1,0:T(1,128)S(1)} %bitcast.4), custom_call_target="tpu_custom_call" | custom-call | tf_op jit(solution)/shard_map/unpack/pallas_call | solution.py:292
  (4 shorter events, 0.0 us)
Async XLA Ops:
  0.6 1.3 %copy-start = (bf16[3,64,3072]{2,1,0:T(8,128)(2,1)S(1)}, bf16[3,64,3072]{2,1,0:T(8,128)(2,1)}, u32[]{:S(2)}) copy-start(bf16[3,64,3072]{2,1,0:T(8,128)(2,1)} %video.3) | copy-start | bytes 3538948
  1.9 0.8 %copy-start.2 = (bf16[3,2,3072]{2,1,0:T(2,128)(2,1)S(1)}, bf16[3,2,3072]{2,1,0:T(2,128)(2,1)}, u32[]{:S(2)}) copy-start(bf16[3,2,3072]{2,1,0:T(2,128)(2,1)} %text.3) | copy-start | bytes 110596
  4.2 5.4 %copy-start.1 = (bf16[3,64,3072]{2,1,0:T(8,128)(2,1)S(1)}, bf16[3,64,3072]{2,1,0:T(8,128)(2,1)}, u32[]{:S(2)}) copy-start(bf16[3,64,3072]{2,1,0:T(8,128)(2,1)} %video.3) | copy-start | bytes 3538948
  4.3 5.4 %copy-start.3 = (bf16[3,2,3072]{2,1,0:T(2,128)(2,1)S(1)}, bf16[3,2,3072]{2,1,0:T(2,128)(2,1)}, u32[]{:S(2)}) copy-start(bf16[3,2,3072]{2,1,0:T(2,128)(2,1)} %text.3) | copy-start | bytes 110596
  4.3 30.7 %all-to-all-start = ((bf16[8,200,384]{2,1,0:T(8,128)(2,1)}), bf16[8,200,384]{2,1,0:T(8,128)(2,1)S(1)}, u32[]{:S(2)}, u32[]{:S(2)}) async-start(bf16[8,200,384]{2,1,0:T(8,128)(2,1)} %pack_own.1), calls=%async_computation | async-start | bytes 2457600 | tf_op jit(solution)/shard_map/all_to_all | solution.py:265
  10.0 16.4 %collective-permute-start = (bf16[136,384]{1,0:T(8,128)(2,1)S(1)}, bf16[136,384]{1,0:T(8,128)(2,1)S(1)}, u32[]{:S(2)}, u32[]{:S(2)}) collective-permute-start(bf16[136,384]{1,0:T(8,128)(2,1)S(1)} %get-tuple-element.10), channel_id=1, source_target_pairs={{0,8},{1,9},{2,10},{3,11},{4,12},{5,13},{6,14},{7,15},{8,0},{9,1},... | collective-permute-start | bytes 313352 | tf_op jit(solution)/shard_map/ppermute | solution.py:264
  12.7 16.3 %collective-permute-start.1 = (bf16[136,384]{1,0:T(8,128)(2,1)S(1)}, bf16[136,384]{1,0:T(8,128)(2,1)S(1)}, u32[]{:S(2)}, u32[]{:S(2)}) collective-permute-start(bf16[136,384]{1,0:T(8,128)(2,1)S(1)} %get-tuple-element.11), channel_id=1, source_target_pairs={{0,9},{1,8},{2,11},{3,10},{4,13},{5,12},{6,15},{7,14},{8,1},{9,0},... | collective-permute-start | bytes 313352 | tf_op jit(solution)/shard_map/ppermute | solution.py:264
  12.9 20.7 %collective-permute-start.2 = (bf16[136,384]{1,0:T(8,128)(2,1)S(1)}, bf16[136,384]{1,0:T(8,128)(2,1)S(1)}, u32[]{:S(2)}, u32[]{:S(2)}) collective-permute-start(bf16[136,384]{1,0:T(8,128)(2,1)S(1)} %get-tuple-element.12), channel_id=1, source_target_pairs={{0,10},{1,11},{2,8},{3,9},{4,14},{5,15},{6,12},{7,13},{8,2},{9,3},... | collective-permute-start | bytes 313352 | tf_op jit(solution)/shard_map/ppermute | solution.py:264
  16.5 20.7 %collective-permute-start.3 = (bf16[136,384]{1,0:T(8,128)(2,1)S(1)}, bf16[136,384]{1,0:T(8,128)(2,1)S(1)}, u32[]{:S(2)}, u32[]{:S(2)}) collective-permute-start(bf16[136,384]{1,0:T(8,128)(2,1)S(1)} %get-tuple-element.13), channel_id=1, source_target_pairs={{0,11},{1,10},{2,9},{3,8},{4,15},{5,14},{6,13},{7,12},{8,3},{9,2},... | collective-permute-start | bytes 313352 | tf_op jit(solution)/shard_map/ppermute | solution.py:264
  16.8 23.2 %collective-permute-start.4 = (bf16[136,384]{1,0:T(8,128)(2,1)S(1)}, bf16[136,384]{1,0:T(8,128)(2,1)S(1)}, u32[]{:S(2)}, u32[]{:S(2)}) collective-permute-start(bf16[136,384]{1,0:T(8,128)(2,1)S(1)} %get-tuple-element.14), channel_id=1, source_target_pairs={{0,12},{1,13},{2,14},{3,15},{4,8},{5,9},{6,10},{7,11},{8,4},{9,5},... | collective-permute-start | bytes 313352 | tf_op jit(solution)/shard_map/ppermute | solution.py:264
  26.5 14.6 %collective-permute-start.5 = (bf16[136,384]{1,0:T(8,128)(2,1)S(1)}, bf16[136,384]{1,0:T(8,128)(2,1)S(1)}, u32[]{:S(2)}, u32[]{:S(2)}) collective-permute-start(bf16[136,384]{1,0:T(8,128)(2,1)S(1)} %get-tuple-element.15), channel_id=1, source_target_pairs={{0,13},{1,12},{2,15},{3,14},{4,9},{5,8},{6,11},{7,10},{8,5},{9,4},... | collective-permute-start | bytes 313352 | tf_op jit(solution)/shard_map/ppermute | solution.py:264
  29.0 16.3 %collective-permute-start.6 = (bf16[136,384]{1,0:T(8,128)(2,1)S(1)}, bf16[136,384]{1,0:T(8,128)(2,1)S(1)}, u32[]{:S(2)}, u32[]{:S(2)}) collective-permute-start(bf16[136,384]{1,0:T(8,128)(2,1)S(1)} %get-tuple-element.16), channel_id=1, source_target_pairs={{0,14},{1,15},{2,12},{3,13},{4,10},{5,11},{6,8},{7,9},{8,6},{9,7},... | collective-permute-start | bytes 313352 | tf_op jit(solution)/shard_map/ppermute | solution.py:264
  33.6 12.8 %collective-permute-start.7 = (bf16[136,384]{1,0:T(8,128)(2,1)S(1)}, bf16[136,384]{1,0:T(8,128)(2,1)S(1)}, u32[]{:S(2)}, u32[]{:S(2)}) collective-permute-start(bf16[136,384]{1,0:T(8,128)(2,1)S(1)} %get-tuple-element.17), channel_id=1, source_target_pairs={{0,15},{1,14},{2,13},{3,12},{4,11},{5,10},{6,9},{7,8},{8,7},{9,6},... | collective-permute-start | bytes 313352 | tf_op jit(solution)/shard_map/ppermute | solution.py:264
  37.2 29.0 %copy-start.4 = (f32[3072]{0:T(1024)S(1)}, f32[3072]{0:T(1024)}, u32[]{:S(2)}) copy-start(f32[3072]{0:T(1024)} %param.6) | copy-start | bytes 36868
  37.2 29.0 %copy-start.5 = (f32[3072]{0:T(1024)S(1)}, f32[3072]{0:T(1024)}, u32[]{:S(2)}) copy-start(f32[3072]{0:T(1024)} %param.7) | copy-start | bytes 36868
